TPU v7x, 256 devices: a 2x2x32 block of a 4x8x32 slice. The times are simulated.
256 devices in a mesh: groups: 4 (over y, x), blk: 32 (over z), sub: 2 (over core).
Axes of the slice: x: 2, y: 2, z: 32, core: 2. Of those that a mesh axis runs over, the one named last changes fastest.
The devices are a block of a 4x8x32 slice.
Arguments:
- embeddings: bfloat16 [49152, 1024], P(('groups', 'blk', 'sub')), parts along dimension 0, may hold values from -6 to 6
- member_key: int32 [49152], P(('groups', 'blk', 'sub')), parts along dimension 0, may hold values from 0 to 1073741823, as said below
- limit_index: int32 [4], P('groups'), parts along dimension 0, may hold values from 0 to 7
Outputs:
- max_cosine: float32 [49152], P(('groups', 'blk', 'sub')), parts along dimension 0
- kept_share: float32 [4], P('groups'), parts along dimension 0
There are 4 independent parts, one for each index of `groups`. A program takes and returns all parts, laid end to end along the dimension named above; each array names one. Nothing has to cross between parts.
Inputs may be any that keep to these rules, and one draw needn't show every extreme that they name: `member_key`: all keys of a cluster are distinct. A key's quotient by 268435456 is the member's sub-cluster, 0 to 3; its remainder orders the members.
All inputs are finite; a program needn't handle non-finite values.
Results may differ from a plain program's by a relative error of at most 0.0013.
Values may be sent and summed in bfloat16 or wider, within the bound.
No kernel may reach another device: no remote copies, remote signals or barrier semaphores. Data moves between devices by JAX's collectives and lax.ppermute only.
A program may use at most 64 MiB of HBM per device.

v0:
```python
import math
import jax
import jax.numpy as jnp
from jax import lax
from jax.sharding import PartitionSpec as P

LIMITS = 8
label_stride = 268435456


def joined_along(pieces, dim):
    dims = list(pieces.shape[1:])
    dims[dim] *= pieces.shape[0]
    return jnp.moveaxis(pieces, 0, dim).reshape(dims)


def all_blocks(shard, axes, turns):
    pieces = shard
    for k in turns:
        pieces = lax.all_gather(pieces, axes[k])
    done = turns[::-1]
    back = [done.index(k) for k in range(len(axes))]
    pieces = pieces.transpose(*back, *range(len(axes), pieces.ndim))
    return pieces.reshape(-1, *shard.shape)


def whole_of(shard, axes, turns, dim):
    return joined_along(all_blocks(shard, axes, turns), dim)


def from_everyone(shard, axis):
    devices = lax.axis_size(axis)
    return lax.all_to_all(
        jnp.broadcast_to(shard[None], (devices, *shard.shape)), axis, 0, 0, tiled=True
    )


def taken_together(shard, axis):
    return from_everyone(shard, axis).sum(axis=0)


def normalize(embeddings):
    values = embeddings.astype(jnp.float32)
    mean_square = jnp.mean(values * values, axis=1, keepdims=True)
    scaled = values * lax.rsqrt(mean_square + 1e-06) * (1.0 / math.sqrt(values.shape[1]))
    return scaled.astype(jnp.bfloat16)


def make_absorb(rows, row_key, key_seen):
    row_label = row_key // label_stride

    def absorb(best, piece, start):
        other_label = key_seen // label_stride
        scores = lax.dot_general(
            rows, piece, (((1,), (1,)), ((), ())), preferred_element_type=jnp.float32
        )
        allowed = (key_seen[None, :] < row_key[:, None]) & (
            other_label[None, :] == row_label[:, None]
        )
        return jnp.maximum(best, jnp.max(jnp.where(allowed, scores, jnp.float32(-1.0)), axis=1))

    return absorb


def on_device(embeddings, member_key, limit_index):
    unit = normalize(embeddings)
    own_rows = unit.shape[0]
    key_all = whole_of(member_key, ("blk", "sub"), (0, 1), 0)
    chip_unit = lax.all_gather(unit, "sub", axis=0, tiled=True)
    core = lax.axis_index("sub")
    begin = lax.axis_index("blk") * (2 * own_rows)
    chip_key = lax.dynamic_slice_in_dim(key_all, begin, 2 * own_rows, 0)
    half_key = lax.dynamic_index_in_dim(
        key_all.reshape(-1, 2, own_rows), core, 1, keepdims=False
    ).reshape(-1)
    absorb = make_absorb(chip_unit, chip_key, half_key)
    start_best = jnp.full((2 * own_rows,), -1.0, jnp.float32)
    half_best = absorb(start_best, lax.all_gather(unit, "blk", axis=0, tiled=True), jnp.int32(0))
    chip_best = lax.pmax(half_best, "sub")
    max_cosine = lax.dynamic_slice_in_dim(chip_best, core * own_rows, own_rows, 0)
    width = math.sqrt(unit.shape[1])
    table = (2.0 + 0.5 * jnp.arange(LIMITS, dtype=jnp.float32)) / width
    limit = jnp.sum(
        jnp.where(jnp.arange(LIMITS, dtype=jnp.int32) == limit_index[0], table, jnp.float32(0.0))
    )
    kept = jax.nn.sigmoid(2.0 * width * (limit - max_cosine))
    kept_sum = taken_together(jnp.sum(kept), ("blk", "sub"))
    kept_share = (kept_sum / key_all.shape[0]).reshape(1)
    return (max_cosine, kept_share)


def solution(mesh):
    in_specs = (P(("groups", "blk", "sub"), None), P(("groups", "blk", "sub")), P("groups"))
    out_specs = (P(("groups", "blk", "sub")), P("groups"))
    return jax.shard_map(
        on_device, mesh=mesh, in_specs=in_specs, out_specs=out_specs, check_vma=False
    )
```

profile of v0, /device:TPU:37, one launch (start us, length us, event | category | flops | bytes accessed | tf_op | source)
XLA Modules:
  0.0 249.5 jit_solution(8639615771263818158)
XLA Ops:
  7.2 0.1 all-gather.4.cloned.1.call-start
  7.2 1.2 fusion
  8.4 1.9 fusion.2
  10.3 0.1 all-gather.4.cloned.1.call-update
  11.1 1.3 dynamic-slice.4
  13.0 0.9 dynamic-update-slice
  13.9 112.4 %all-reduce = s32[6144]{0:T(1024)S(1)} all-reduce(s32[6144]{0:T(1024)S(1)} %dynamic-update-slice), channel_id=2, replica_groups=mesh['groups'=4,'blk'=32,'sub'=2] {'blk'}, use_global_device_ids=true, to_apply=%add | all-reduce | flops 6144 | bytes 49152
  126.2 0.1 reshape.56
  126.3 19.7 %all-gather.1 = s32[64,192]{1,0:T(8,128)S(1)} all-gather(s32[32,192]{1,0:T(8,128)S(1)} %reshape.56), channel_id=3, replica_groups=mesh['groups'=4,'blk'=32,'sub'=2] {'sub'}, dimensions={0}, use_global_device_ids=true | all-gather | bytes 73728 | tf_op jit(solution)/shard_map/all_gather | solution.py:20
  146.1 0.1 lt.26
  146.2 0.1 copy.7
  146.2 0.1 reshape_reshape.3
  146.3 0.7 fusion.8
  147.0 0.1 add_select_fusion.1
  147.1 2.6 %all_gather.22 = bf16[384,1024]{1,0:T(8,128)(2,1)S(1)} all-gather(bf16[192,1024]{1,0:T(8,128)(2,1)} %fusion.2), channel_id=1, replica_groups=mesh['groups'=4,'blk'=32,'sub'=2] {'sub'}, dimensions={0}, use_global_device_ids=true | all-gather | bytes 1179648 | tf_op jit(solution)/shard_map/all_gather | solution.py:69
  149.7 31.2 %all-gather.4.cloned.1.call-done = bf16[6144,1024]{1,0:T(8,128)(2,1)} async-done(((bf16[192,1024]{1,0:T(8,128)(2,1)}), bf16[6144,1024]{1,0:T(8,128)(2,1)}) %all-gather.4.cloned.1.call-update) | async-done | bytes 12582928 | tf_op jit(solution)/shard_map/all_gather | solution.py:78
  180.9 8.7 %select_reduce_fusion = f32[384]{0:T(512)S(1)} fusion(bf16[384,1024]{1,0:T(8,128)(2,1)S(1)} %all_gather.22, bf16[6144,1024]{1,0:T(8,128)(2,1)} %all-gather.4.cloned.1.call-done, s32[6144]{0:T(1024)S(1)} %add_select_fusion, s32[6144]{0:T(1024)S(1)} %lt.26, s32[384]{0:T(512)S(1)} %get-tuple-element.4, s32[384]{0:T(512)S(1)} %get-tuple-element.5), kind=kOutput, calls=%fused_computation | convolution fusion | flops 4843634176 | bytes 13423104 | tf_op jit(solution)/shard_map/dot_general | solution.py:54
  189.6 10.0 %pmax.7 = f32[384]{0:T(512)S(1)} all-reduce(f32[384]{0:T(512)S(1)} %broadcast_maximum_fusion), channel_id=1, replica_groups=mesh['groups'=4,'blk'=32,'sub'=2] {'sub'}, use_global_device_ids=true, to_apply=%region_2.3 | all-reduce | flops 384 | bytes 3072 | tf_op jit(solution)/shard_map/pmax | solution.py:79
  199.7 1.9 fusion.7
  201.6 0.7 broadcast_in_dim.24
  202.2 38.0 %all_to_all.6 = f32[64,1,1]{2,1,0:T(1,128)S(1)} all-to-all(f32[64,1,1]{2,1,0:T(1,128)S(1)} %broadcast_in_dim.24), channel_id=1, replica_groups=mesh['groups'=4,'blk'=32,'sub'=2] {'blk','sub'}, dimensions={0} | all-to-all | bytes 512 | tf_op jit(solution)/shard_map/all_to_all | solution.py:33
  240.2 0.7 reduce_sum.39
  (5 shorter events, 0.0 us)
Async XLA Ops:
  7.2 173.7 %all-gather.4.cloned.1.call-start = ((), (), s32[]{:S(2)}) async-start(), calls=%async_computation.1 | async-start | bytes 12976128 | tf_op jit(solution)/shard_map/all_gather | solution.py:78
Sparse Core Ops, SparseCore 0:
  10.5 170.3 all-gather.3
where the time goes:
time: 250 us
  blocking collectives  183 us (73%)
  waiting for transfers between devices  31.3 us (13%)
  between operations  17.2 us (7%)
  matrix products  8.69 us (3%)
  other arithmetic  6.44 us (3%)
  local copies, waits for them, and re-layouts  3.14 us (1%)
    unnamed x1, blocking collectives  112 us
    all_to_all x1, blocking collectives, from_everyone(): lax.all_to_all(jnp.broadcast_to(shard[None], (devices, *shard.shape)), ax...  38 us
    all_gather x1, waiting for transfers between devices, on_device(): lax.all_gather(unit, 'blk', axis=0, tiled=True)  31.2 us
    all_gather x1, blocking collectives, all_blocks(): pieces = lax.all_gather(pieces, axes[k])  19.7 us
    pmax x1, blocking collectives, on_device(): chip_best = lax.pmax(half_best, 'sub')  10 us
    dot_general x1, matrix products, absorb(): lax.dot_general(rows, piece, (((1,), (1,)), ((), ())), preferred_element_...  8.69 us
  transfers between devices with their start and end apart: 1, of which 1 were waited for; matrix products, arithmetic and copies ran while one was open for 1% of the time, Pallas kernels for 0%

commit v1 on v0

--- a/solution.py
+++ b/solution.py
@@ -6,6 +6,12 @@
 
 LIMITS = 8
 label_stride = 268435456
+
+
+def tiled_gather(x, axis, dim):
+    size = lax.axis_size(axis)
+    repeats = [size if d == dim else 1 for d in range(x.ndim)]
+    return lax.all_to_all(jnp.tile(x, repeats), axis, split_axis=dim, concat_axis=dim, tiled=True)
 
 
 def joined_along(pieces, dim):
@@ -75,7 +81,7 @@
     ).reshape(-1)
     absorb = make_absorb(chip_unit, chip_key, half_key)
     start_best = jnp.full((2 * own_rows,), -1.0, jnp.float32)
-    half_best = absorb(start_best, lax.all_gather(unit, "blk", axis=0, tiled=True), jnp.int32(0))
+    half_best = absorb(start_best, tiled_gather(unit, "blk", 0), jnp.int32(0))
     chip_best = lax.pmax(half_best, "sub")
     max_cosine = lax.dynamic_slice_in_dim(chip_best, core * own_rows, own_rows, 0)
     width = math.sqrt(unit.shape[1])

time: 250 us -> 1290 us (5.16)
  blocking collectives: 183 us -> 1230 us
  starting transfers between devices: 0.06 us -> 33.3 us
  waiting for transfers between devices: 31.3 us -> 0.01 us
  between operations: 17.2 us -> 3.8 us
    unnamed x1, blocking collectives: 112 us -> 1160 us
    all_to_all x0 -> x1, starting transfers between devices: none -> 33.3 us  [tiled_gather(): lax.all_to_all(jnp.tile(x, repeats), axis, split_axis=dim, concat_axis=di...]
    all_gather x1 -> x0, waiting for transfers between devices: 31.2 us -> none  [on_device(): lax.all_gather(unit, 'blk', axis=0, tiled=True)]
  transfers between devices with their start and end apart: 1 -> 1, of which waited for: 1 -> 0; matrix products, arithmetic and copies ran while one was open for 1% -> 0% of each run, Pallas kernels for 0% -> 0%
where the time goes in v1:
time: 1290 us
  blocking collectives  1230 us (95%)
  starting transfers between devices  33.3 us (3%)
    unnamed x1, blocking collectives  1160 us
    all_to_all x1, blocking collectives, from_everyone(): lax.all_to_all(jnp.broadcast_to(shard[None], (devices, *shard.shape)), ax...  41 us
    all_to_all x1, starting transfers between devices, tiled_gather(): lax.all_to_all(jnp.tile(x, repeats), axis, split_axis=dim, concat_axis=di...  33.3 us
    all_gather x1, blocking collectives, all_blocks(): pieces = lax.all_gather(pieces, axes[k])  26.7 us
  transfers between devices with their start and end apart: 1, of which 0 were waited for; matrix products, arithmetic and copies ran while one was open for 0% of the time, Pallas kernels for 0%

profile of v1, /device:TPU:37, one launch (start us, length us, event | category | flops | bytes accessed | tf_op | source)
XLA Modules:
  0.0 1288.5 jit_solution(4841362693350113522)
XLA Ops:
  0.6 1.2 fusion
  1.8 1.2 fusion.2
  3.0 6.1 tile.2
  9.0 33.3 %all-to-all-start = ((bf16[32,192,1024]{2,1,0:T(8,128)(2,1)}), bf16[32,192,1024]{2,1,0:T(8,128)(2,1)}, u32[]{:S(2)}, u32[]{:S(2)}) async-start(bf16[32,192,1024]{2,1,0:T(8,128)(2,1)} %tile.2), calls=%async_computation | async-start | bytes 25165824 | tf_op jit(solution)/shard_map/all_to_all | solution.py:14
  42.4 0.0 copy-done.1
  42.4 0.6 dynamic-slice.4
  43.7 0.0 copy-done
  43.7 0.3 dynamic-update-slice
  44.0 1156.5 %all-reduce = s32[6144]{0:T(1024)S(1)} all-reduce(s32[6144]{0:T(1024)S(1)} %dynamic-update-slice), channel_id=2, replica_groups=mesh['groups'=4,'blk'=32,'sub'=2] {'blk'}, use_global_device_ids=true, to_apply=%add | all-reduce | flops 6144 | bytes 49152
  1200.5 0.1 reshape.63
  1200.6 26.7 %all-gather.1 = s32[64,192]{1,0:T(8,128)S(1)} all-gather(s32[32,192]{1,0:T(8,128)S(1)} %reshape.63), channel_id=3, replica_groups=mesh['groups'=4,'blk'=32,'sub'=2] {'sub'}, dimensions={0}, use_global_device_ids=true | all-gather | bytes 73728 | tf_op jit(solution)/shard_map/all_gather | solution.py:26
  1227.3 0.1 lt.26
  1227.4 0.1 copy.7
  1227.4 0.1 reshape_reshape.3
  1228.2 0.6 fusion.8
  1228.8 0.1 add_select_fusion.1
  1228.9 2.4 all_gather.19
  1231.3 0.0 all-to-all-done
  1231.3 8.7 select_reduce_fusion
  1240.0 2.5 pmax.7
  1242.6 1.9 fusion.7
  1244.4 0.7 broadcast_in_dim.24
  1245.1 41.0 %all_to_all.15 = f32[64,1,1]{2,1,0:T(1,128)S(1)} all-to-all(f32[64,1,1]{2,1,0:T(1,128)S(1)} %broadcast_in_dim.24), channel_id=1, replica_groups=mesh['groups'=4,'blk'=32,'sub'=2] {'blk','sub'}, dimensions={0} | all-to-all | bytes 512 | tf_op jit(solution)/shard_map/all_to_all | solution.py:39
  1286.1 0.7 reduce_sum.39
  (7 shorter events, 0.0 us)
Async XLA Ops:
  9.0 33.4 %copy-start.1 = (u32[256]{0:T(256)S(1)}, u32[256]{0:T(256)}, u32[]{:S(2)}) copy-start(u32[256]{0:T(256)} %constant.77) | copy-start | bytes 3076
  9.0 34.6 %copy-start = (s32[192]{0:T(256)S(1)}, s32[192]{0:T(256)}, u32[]{:S(2)}) copy-start(s32[192]{0:T(256)} %param.4) | copy-start | bytes 2308
  9.0 1222.3 %all-to-all-start = ((bf16[32,192,1024]{2,1,0:T(8,128)(2,1)}), bf16[32,192,1024]{2,1,0:T(8,128)(2,1)}, u32[]{:S(2)}, u32[]{:S(2)}) async-start(bf16[32,192,1024]{2,1,0:T(8,128)(2,1)} %tile.2), calls=%async_computation | async-start | bytes 25165824 | tf_op jit(solution)/shard_map/all_to_all | solution.py:14
